TPU v7x, 32 devices: a whole 2x2x4 slice. The times are simulated.
32 devices in a mesh: row: 8 (over y, x, core), col: 4 (over z).
Axes of the slice: x: 2, y: 2, z: 4, core: 2. Of those that a mesh axis runs over, the one named last changes fastest.
Arguments:
- species: float32 [2, 256, 256, 128], P(None, None, 'row', 'col'), may hold values from -6 to 6
- coupling: float32 [2, 2], replicated, may hold values from -4 to 4
- symbol_x: float32 [256], replicated, may hold values from 0.3 to 3
- symbol_y: float32 [256], replicated, may hold values from 0.3 to 3
- symbol_z: float32 [128], replicated, may hold values from 0.3 to 3
Outputs:
- modes: float32 [2, 256, 256, 128], P(None, 'row', 'col')
All inputs are finite; a program needn't handle non-finite values.
Results may differ from a plain program's by a relative error of at most 0.000078.
Values sent between devices are 32-bit elements.
A program may use at most 128 MiB of HBM per device.

v0:
```python
import functools

import jax
import jax.numpy as jnp
import numpy as np
from jax import lax
from jax.experimental import pallas as pl
from jax.experimental.pallas import tpu as pltpu
from jax.sharding import PartitionSpec as P

MESH = pl.DeviceIdType.MESH
LANES = 128
SUB = 8


def mode_table(count):
    rank = np.arange(1, count + 1)
    angle = np.pi / (count + 1) * ((rank[:, None] * rank[None, :]) % (2 * count + 2))
    return (np.sin(angle) * np.sqrt(2.0 / (count + 1))).astype(np.float32)


def halves_of(table):
    high = table.astype(jnp.bfloat16)
    low = (table - high.astype(np.float32)).astype(jnp.bfloat16)
    return high, low


def halves(values):
    high = values.astype(jnp.bfloat16)
    low = (values - high.astype(jnp.float32)).astype(jnp.bfloat16)
    return high, low


def partner(me, step, count):
    if count & (count - 1):
        return lax.rem(me + step, count)
    other, bit = me, 1
    while bit < count:
        if step & bit:
            other = other + bit * (1 - 2 * lax.rem(me // bit, 2))
        bit *= 2
    return other


def swap_groups(parts):
    parts = list(parts)
    count = len(parts)
    width = LANES // count
    lane = lax.broadcasted_iota(jnp.int32, parts[0].shape, 1)
    step = count // 2
    while step:
        keep = lax.rem(lane // (width * step), 2) == 0
        for first in range(count):
            if first & step:
                continue
            a, b = parts[first], parts[first + step]
            parts[first] = jnp.where(keep, a, pltpu.roll(b, width * step, 1))
            parts[first + step] = jnp.where(keep, pltpu.roll(a, LANES - width * step, 1), b)
        step //= 2
    return parts


def kernel(sizes, a_ref, hx_ref, hy_ref, hz_ref, o_ref, t_ref, r_ref, v_ref, w_ref,
           send_row, recv_row, send_col, recv_col, own_row, own_col):
    rows, cols, fields, nx, ny, nz = sizes
    share_y = ny // cols
    groups = LANES // (nz // cols)
    blocks = ny // rows // groups
    chunks = nx // rows // SUB
    quads = SUB // groups
    total = fields * chunks
    slab = blocks * SUB
    row, col = lax.axis_index("row"), lax.axis_index("col")

    barrier = pltpu.get_barrier_semaphore()
    for step in range(1, rows):
        pl.semaphore_signal(barrier, inc=1, device_id={"row": partner(row, step, rows)}, device_id_type=MESH)
    for step in range(1, cols):
        pl.semaphore_signal(barrier, inc=1, device_id={"col": partner(col, step, cols)}, device_id_type=MESH)

    def row_copy(i, step):
        to = partner(row, step, rows)
        return pltpu.make_async_remote_copy(
            src_ref=t_ref.at[i, to], dst_ref=r_ref.at[i, pl.ds(row * slab, slab)],
            send_sem=send_row.at[i, step], recv_sem=recv_row.at[i, step],
            device_id={"row": to}, device_id_type=MESH)

    def own_row_copy(i):
        return pltpu.make_async_copy(
            t_ref.at[i, row], r_ref.at[i, pl.ds(row * slab, slab)], own_row.at[i])

    def col_copy(i, step):
        to = partner(col, step, cols)
        return pltpu.make_async_remote_copy(
            src_ref=v_ref.at[i, to], dst_ref=w_ref.at[i, col],
            send_sem=send_col.at[i, step], recv_sem=recv_col.at[i, step],
            device_id={"col": to}, device_id_type=MESH)

    def own_col_copy(i):
        return pltpu.make_async_copy(v_ref.at[i, col], w_ref.at[i, col], own_col.at[i])

    per_dot = 2
    for f in range(fields):
        for n in range(blocks // per_dot):
            width = per_dot * LANES
            high, low = halves(a_ref[f, n * width:(n + 1) * width, :])
            part = lax.dot_general(
                hx_ref[...], jnp.concatenate([high, high, low], axis=1),
                (((1,), (1,)), ((), ())), preferred_element_type=jnp.float32)
            part = part.reshape(rows, chunks, SUB, width)
            for j in range(chunks):
                for b in range(per_dot):
                    at = (n * per_dot + b) * SUB
                    t_ref[f * chunks + j, :, at:at + SUB, :] = part[:, j, :, b * LANES:(b + 1) * LANES]
        if f == 0:
            pl.semaphore_wait(barrier, rows + cols - 2)
        for j in range(chunks):
            for step in range(rows - 1, 0, -1):
                row_copy(f * chunks + j, step).start()
            own_row_copy(f * chunks + j).start()

    def y_step(i, carry):
        for step in range(rows - 1, 0, -1):
            row_copy(i, step).wait_recv()
        own_row_copy(i).wait()
        whole = []
        for q in range(quads):
            parts = [r_ref[i, pl.ds(q * groups + g, rows * blocks, stride=SUB), :] for g in range(groups)]
            whole.append(jnp.concatenate(swap_groups(parts), axis=0))
        high, low = halves(jnp.concatenate(whole, axis=1))
        got = jnp.dot(hy_ref[...], jnp.concatenate([high, high, low], axis=0),
                      preferred_element_type=jnp.float32)
        for c in range(cols):
            for q in range(quads):
                v_ref[i, c, q * share_y:(q + 1) * share_y, :] = got[
                    c * share_y:(c + 1) * share_y, q * LANES:(q + 1) * LANES]
        for step in range(cols - 1, 0, -1):
            col_copy(i, step).start()
        own_col_copy(i).start()
        return carry

    lax.fori_loop(0, total, y_step, 0)

    def z_step(i, carry):
        for step in range(cols - 1, 0, -1):
            col_copy(i, step).wait_recv()
        own_col_copy(i).wait()
        lines = []
        for q in range(quads):
            tiles = []
            for c in range(0, cols, groups):
                tiles.append(swap_groups(
                    [w_ref[i, c + g, q * share_y:(q + 1) * share_y, :] for g in range(groups)]))
            for k in range(groups):
                lines.append(jnp.concatenate([tile[k] for tile in tiles], axis=1))
        high, low = halves(jnp.concatenate(lines, axis=0))
        got = jnp.dot(jnp.concatenate([high, low], axis=1), hz_ref[...],
                      preferred_element_type=jnp.float32)
        got = (got[:, :nz] + got[:, nz:]).reshape(SUB, share_y, nz)
        o_ref[i // chunks, pl.ds(lax.rem(i, chunks) * SUB, SUB)] = got
        return carry

    lax.fori_loop(0, total, z_step, 0)

    def drain(i, carry):
        for step in range(1, rows):
            row_copy(i, step).wait_send()
        for step in range(1, cols):
            col_copy(i, step).wait_send()
        return carry

    lax.fori_loop(0, total, drain, 0)


def local(rows, cols, species, coupling, symbol_x, symbol_y, symbol_z):
    fields, nx, near_y, near_z = species.shape
    ny, nz = near_y * rows, near_z * cols
    share_x, share_y = nx // rows, ny // cols
    groups = LANES // near_z
    blocks = near_y // groups
    total = fields * share_x // SUB

    high, low = halves_of(mode_table(nx))
    hx = np.concatenate([high, low, high], axis=1)
    order = np.arange(ny).reshape(rows, blocks, groups).transpose(2, 0, 1).reshape(-1)
    high, low = halves_of(mode_table(ny)[:, order])
    hy = np.concatenate([high, low, high], axis=1)
    high, low = halves_of(mode_table(nz))
    hz = np.concatenate([np.concatenate([high, low], axis=1),
                         np.concatenate([high, np.zeros_like(low)], axis=1)], axis=0)

    lines = jnp.transpose(species, (0, 2, 3, 1)).reshape(fields, near_y * near_z, nx)
    vmem = pl.BlockSpec(memory_space=pltpu.VMEM)
    dma = pltpu.SemaphoreType.DMA
    modes = pl.pallas_call(
        functools.partial(kernel, (rows, cols, fields, nx, ny, nz)),
        out_shape=jax.ShapeDtypeStruct((fields, share_x, share_y, nz), jnp.float32),
        in_specs=[vmem] * 4,
        out_specs=vmem,
        scratch_shapes=[
            pltpu.VMEM((total, rows, blocks * SUB, LANES), jnp.float32),
            pltpu.VMEM((total, rows * blocks * SUB, LANES), jnp.float32),
            pltpu.VMEM((total, cols, SUB // groups * share_y, LANES), jnp.float32),
            pltpu.VMEM((total, cols, SUB // groups * share_y, LANES), jnp.float32),
            dma((total, rows)), dma((total, rows)),
            dma((total, cols)), dma((total, cols)),
            dma((total,)), dma((total,)),
        ],
        compiler_params=pltpu.CompilerParams(
            collective_id=0, has_side_effects=True, vmem_limit_bytes=56 * 2**20),
    )(lines, jnp.asarray(hx), jnp.asarray(hy), jnp.asarray(hz))

    part_x = lax.dynamic_slice_in_dim(symbol_x, lax.axis_index("row") * share_x, share_x)
    part_y = lax.dynamic_slice_in_dim(symbol_y, lax.axis_index("col") * share_y, share_y)
    symbol = part_x[:, None, None] + part_y[None, :, None] + symbol_z[None, None, :]
    weight = 1.0 / (1.0 + symbol)
    mixed = sum(coupling[:, b, None, None, None] * modes[b][None] for b in range(fields))
    return weight * modes + (1.0 - weight) * mixed


def solution(mesh):
    return jax.shard_map(
        functools.partial(local, mesh.shape["row"], mesh.shape["col"]),
        mesh=mesh,
        in_specs=(P(None, None, "row", "col"), P(), P(), P(), P()),
        out_specs=P(None, "row", "col", None),
        check_vma=False,
    )
```

profile of v0, /device:TPU:0, one launch (start us, length us, event | category | flops | bytes accessed | tf_op | source)
XLA Modules:
  0.0 71.0 jit_solution(12087965846228168532)
XLA Ops:
  0.0 0.8 %dynamic_slice.7 = f32[64]{0:T(128)S(1)} dynamic-slice(f32[256]{0:T(256)} %param.11, s32[]{:T(128)S(6)} %select_n.7), dynamic_slice_sizes={64} | dynamic-slice | bytes 516 | tf_op jit(solution)/shard_map/dynamic_slice | solution.py:214
  0.8 0.8 %dynamic_slice.6 = f32[32]{0:T(128)S(1)} dynamic-slice(f32[256]{0:T(256)} %param.10, s32[]{:T(128)S(6)} %select_n.6), dynamic_slice_sizes={32} | dynamic-slice | bytes 260 | tf_op jit(solution)/shard_map/dynamic_slice | solution.py:213
  1.5 1.0 %slice_reduce_fusion.1 = (f32[2]{0:T(128)S(1)}, f32[2]{0:T(128)S(1)}) fusion(f32[2,2]{1,0:T(2,128)} %param.9), kind=kLoop, calls=%fused_computation.7 | loop fusion | bytes 32 | tf_op jit(solution)/shard_map/slice | solution.py:217
  2.5 0.1 broadcast_add_fusion
  2.5 1.0 %add_divide_fusion = (f32[32,64,128]{2,1,0:T(8,128)S(1)}, f32[32,64,128]{2,1,0:T(8,128)S(1)}) fusion(f32[128]{0:T(128)} %param.12, f32[32,64]{1,0:T(8,128)S(1)} %broadcast_add_fusion), kind=kLoop, calls=%fused_computation.3 | loop fusion | flops 1048576 | bytes 2105856 | tf_op jit(solution)/shard_map/div | solution.py:216
  3.6 63.1 %shard_map.82 = f32[2,32,64,128]{3,2,1,0:T(8,128)} custom-call(f32[2,1024,256]{2,1,0:T(8,128)} %bitcast.7, bf16[256,768]{1,0:T(8,128)(2,1)} %constant.25.clone.hx_ref, bf16[256,768]{1,0:T(8,128)(2,1)} %constant.26.clone.hy_ref, bf16[256,256]{1,0:T(8,128)(2,1)} %constant.27.clone.hz_ref), custom_call_target="tpu_custom_call" | custom-call | tf_op jit(solution)/shard_map/pallas_call | solution.py:195
  66.7 0.0 copy-start
  66.7 1.9 %slice_bitcast_fusion.1 = (f32[32,64,128]{2,1,0:T(8,128)S(1)}, f32[32,64,128]{2,1,0:T(8,128)S(1)}) fusion(f32[2,32,64,128]{3,2,1,0:T(8,128)} %shard_map.82), kind=kLoop, calls=%fused_computation.2 | loop fusion | bytes 4194304 | tf_op jit(solution)/shard_map/mul | solution.py:217
  68.6 0.3 copy-done
  68.9 2.1 %multiply_add_fusion = f32[2,32,64,128]{3,2,1,0:T(8,128)} fusion(f32[2,32,64,128]{3,2,1,0:T(8,128)S(1)} %copy-done, f32[32,64,128]{2,1,0:T(8,128)S(1)} %get-tuple-element.8, f32[2]{0:T(128)S(1)} %get-tuple-element.6, f32[32,64,128]{2,1,0:T(8,128)S(1)} %get-tuple-element.7, f32[2]{0:T(128)S(1)} %get-tuple-element.5, f32[32,64,128]{2,1,0:T(8,128)S(1)} %get-tuple-element.10, ...), kind=kLoop, calls=%fused_computation | loop fusion | flops 3145728 | bytes 8388624 | tf_op jit(solution)/shard_map/add | solution.py:218
Async XLA Ops:
  66.7 2.2 %copy-start = (f32[2,32,64,128]{3,2,1,0:T(8,128)S(1)}, f32[2,32,64,128]{3,2,1,0:T(8,128)}, u32[]{:S(2)}) copy-start(f32[2,32,64,128]{3,2,1,0:T(8,128)} %shard_map.82) | copy-start | bytes 6291460
where the time goes:
time: 71.2 us; the launch traced here: 71 us
  Pallas kernels  63.1 us (89%)
  local copies, waits for them, and re-layouts  4.67 us (7%)
  other arithmetic  3.17 us (4%)
    pallas_call x1, Pallas kernels, local(): pl.pallas_call(functools.partial(kernel, (rows, cols, fields, nx, ny, nz)...  63.1 us
    add x1, other arithmetic, local(): return weight * modes + (1.0 - weight) * mixed  2.09 us
    mul x1, local copies, waits for them, and re-layouts, local(): coupling[:, b, None, None, None] * modes[b][None]  1.93 us

commit v1 on v0

--- a/solution.py
+++ b/solution.py
@@ -60,8 +60,9 @@
     return parts
 
 
-def kernel(sizes, a_ref, hx_ref, hy_ref, hz_ref, o_ref, t_ref, r_ref, v_ref, w_ref,
-           send_row, recv_row, send_col, recv_col, own_row, own_col):
+def kernel(sizes, coupling_ref, sx_ref, a_hbm, hx_hbm, hy_hbm, hz_hbm, sy_ref, sz_ref, o_hbm,
+           a_ref, hx_ref, hy_ref, hz_ref, sy_rows, m_ref, o_ref, t_ref, r_ref, v_ref, w_ref,
+           load_a, load_h, store_o, send_row, recv_row, send_col, recv_col, own_row, own_col):
     rows, cols, fields, nx, ny, nz = sizes
     share_y = ny // cols
     groups = LANES // (nz // cols)
@@ -71,6 +72,22 @@
     total = fields * chunks
     slab = blocks * SUB
     row, col = lax.axis_index("row"), lax.axis_index("col")
+    per_dot = 2
+    width = per_dot * LANES
+    pieces = blocks // per_dot
+
+    def load(f, n):
+        at = pl.ds(n * width, width)
+        return pltpu.make_async_copy(a_hbm.at[f, at], a_ref.at[f, at], load_a.at[f, n])
+
+    tables = [pltpu.make_async_copy(src, dst, load_h.at[n]) for n, (src, dst) in enumerate(
+        ((hx_hbm, hx_ref), (hy_hbm, hy_ref), (hz_hbm, hz_ref)))]
+    tables[0].start()
+    for f in range(fields):
+        for n in range(pieces):
+            load(f, n).start()
+    tables[1].start()
+    tables[2].start()
 
     barrier = pltpu.get_barrier_semaphore()
     for step in range(1, rows):
@@ -99,10 +116,10 @@
     def own_col_copy(i):
         return pltpu.make_async_copy(v_ref.at[i, col], w_ref.at[i, col], own_col.at[i])
 
-    per_dot = 2
+    tables[0].wait()
     for f in range(fields):
-        for n in range(blocks // per_dot):
-            width = per_dot * LANES
+        for n in range(pieces):
+            load(f, n).wait()
             high, low = halves(a_ref[f, n * width:(n + 1) * width, :])
             part = lax.dot_general(
                 hx_ref[...], jnp.concatenate([high, high, low], axis=1),
@@ -118,6 +135,8 @@
             for step in range(rows - 1, 0, -1):
                 row_copy(f * chunks + j, step).start()
             own_row_copy(f * chunks + j).start()
+
+    tables[1].wait()
 
     def y_step(i, carry):
         for step in range(rows - 1, 0, -1):
@@ -141,7 +160,12 @@
 
     lax.fori_loop(0, total, y_step, 0)
 
-    def z_step(i, carry):
+    tables[2].wait()
+    for n in range(ny // LANES):
+        at = slice(n * LANES, (n + 1) * LANES)
+        sy_rows[at, :] = jnp.broadcast_to(sy_ref[:, at], (LANES, LANES)).T
+
+    def modes_of(i):
         for step in range(cols - 1, 0, -1):
             col_copy(i, step).wait_recv()
         own_col_copy(i).wait()
@@ -156,11 +180,35 @@
         high, low = halves(jnp.concatenate(lines, axis=0))
         got = jnp.dot(jnp.concatenate([high, low], axis=1), hz_ref[...],
                       preferred_element_type=jnp.float32)
-        got = (got[:, :nz] + got[:, nz:]).reshape(SUB, share_y, nz)
-        o_ref[i // chunks, pl.ds(lax.rem(i, chunks) * SUB, SUB)] = got
-        return carry
-
-    lax.fori_loop(0, total, z_step, 0)
+        return got[:, :nz] + got[:, nz:]
+
+    def z_step(i, carry):
+        m_ref[i] = modes_of(i)
+        return carry
+
+    lax.fori_loop(0, total - chunks, z_step, 0)
+
+    def store(j):
+        at = pl.ds(j * SUB, SUB)
+        return pltpu.make_async_copy(o_ref.at[:, at], o_hbm.at[:, at], store_o.at[j])
+
+    def last_step(j, carry):
+        last = modes_of(total - chunks + j)
+        lines_y = sy_rows[pl.ds(col * share_y, share_y), :]
+        lines_y = jnp.concatenate([lines_y] * (nz // LANES), axis=1) + sz_ref[...]
+        for k in range(SUB):
+            at = slice(k * share_y, (k + 1) * share_y)
+            weight = 1.0 / (1.0 + (sx_ref[row * (chunks * SUB) + j * SUB + k] + lines_y))
+            old = [m_ref[f * chunks + j, at, :] for f in range(fields - 1)] + [last[at, :]]
+            for f in range(fields):
+                mixed = coupling_ref[f, 0] * old[0]
+                for b in range(1, fields):
+                    mixed = mixed + coupling_ref[f, b] * old[b]
+                o_ref[f, j * SUB + k] = weight * old[f] + (1.0 - weight) * mixed
+        store(j).start()
+        return carry
+
+    lax.fori_loop(0, chunks, last_step, 0)
 
     def drain(i, carry):
         for step in range(1, rows):
@@ -170,6 +218,8 @@
         return carry
 
     lax.fori_loop(0, total, drain, 0)
+    for j in range(chunks):
+        store(j).wait()
 
 
 def local(rows, cols, species, coupling, symbol_x, symbol_y, symbol_z):
@@ -191,31 +241,37 @@
 
     lines = jnp.transpose(species, (0, 2, 3, 1)).reshape(fields, near_y * near_z, nx)
     vmem = pl.BlockSpec(memory_space=pltpu.VMEM)
+    smem = pl.BlockSpec(memory_space=pltpu.SMEM)
+    hbm = pl.BlockSpec(memory_space=pltpu.HBM)
     dma = pltpu.SemaphoreType.DMA
-    modes = pl.pallas_call(
+    f32 = jnp.float32
+    chunks = total // fields
+    return pl.pallas_call(
         functools.partial(kernel, (rows, cols, fields, nx, ny, nz)),
-        out_shape=jax.ShapeDtypeStruct((fields, share_x, share_y, nz), jnp.float32),
-        in_specs=[vmem] * 4,
-        out_specs=vmem,
+        out_shape=jax.ShapeDtypeStruct((fields, share_x, share_y, nz), f32),
+        in_specs=[smem, smem, hbm, hbm, hbm, hbm, vmem, vmem],
+        out_specs=hbm,
         scratch_shapes=[
-            pltpu.VMEM((total, rows, blocks * SUB, LANES), jnp.float32),
-            pltpu.VMEM((total, rows * blocks * SUB, LANES), jnp.float32),
-            pltpu.VMEM((total, cols, SUB // groups * share_y, LANES), jnp.float32),
-            pltpu.VMEM((total, cols, SUB // groups * share_y, LANES), jnp.float32),
+            pltpu.VMEM(lines.shape, f32),
+            pltpu.VMEM(hx.shape, hx.dtype),
+            pltpu.VMEM(hy.shape, hy.dtype),
+            pltpu.VMEM(hz.shape, hz.dtype),
+            pltpu.VMEM((ny, LANES), f32),
+            pltpu.VMEM((max(total - chunks, 1), SUB * share_y, nz), f32),
+            pltpu.VMEM((fields, share_x, share_y, nz), f32),
+            pltpu.VMEM((total, rows, blocks * SUB, LANES), f32),
+            pltpu.VMEM((total, rows * blocks * SUB, LANES), f32),
+            pltpu.VMEM((total, cols, SUB // groups * share_y, LANES), f32),
+            pltpu.VMEM((total, cols, SUB // groups * share_y, LANES), f32),
+            dma((fields, blocks // 2)), dma((3,)), dma((chunks,)),
             dma((total, rows)), dma((total, rows)),
             dma((total, cols)), dma((total, cols)),
             dma((total,)), dma((total,)),
         ],
         compiler_params=pltpu.CompilerParams(
-            collective_id=0, has_side_effects=True, vmem_limit_bytes=56 * 2**20),
-    )(lines, jnp.asarray(hx), jnp.asarray(hy), jnp.asarray(hz))
-
-    part_x = lax.dynamic_slice_in_dim(symbol_x, lax.axis_index("row") * share_x, share_x)
-    part_y = lax.dynamic_slice_in_dim(symbol_y, lax.axis_index("col") * share_y, share_y)
-    symbol = part_x[:, None, None] + part_y[None, :, None] + symbol_z[None, None, :]
-    weight = 1.0 / (1.0 + symbol)
-    mixed = sum(coupling[:, b, None, None, None] * modes[b][None] for b in range(fields))
-    return weight * modes + (1.0 - weight) * mixed
+            collective_id=0, has_side_effects=True, vmem_limit_bytes=60 * 2**20),
+    )(coupling, symbol_x, lines, jnp.asarray(hx), jnp.asarray(hy), jnp.asarray(hz),
+      symbol_y[None, :], symbol_z[None, :])
 
 
 def solution(mesh):

time: 71.2 us -> 65.7 us (0.923)
  other arithmetic: 3.17 us -> 0 us
  local copies, waits for them, and re-layouts: 4.67 us -> 3.16 us
    unnamed x2 -> x1, local copies, waits for them, and re-layouts: 0.28 us -> 3.16 us
    add x2 -> x0, other arithmetic: 2.16 us -> none  [the longest x1 2.09 us: local(): return weight * modes + (1.0 - weight) * mixed]
    mul x1 -> x0, local copies, waits for them, and re-layouts: 1.93 us -> none  [local(): coupling[:, b, None, None, None] * modes[b][None]]
    dynamic_slice x2 -> x0, local copies, waits for them, and re-layouts: 1.5 us -> none  [the longest x1 0.75 us: local(): lax.dynamic_slice_in_dim(symbol_y, lax.axis_index('col') * share_y, share_y)]
    div x1 -> x0, other arithmetic: 1.01 us -> none  [local(): weight = 1.0 / (1.0 + symbol)]
    slice x1 -> x0, local copies, waits for them, and re-layouts: 0.96 us -> none  [local(): coupling[:, b, None, None, None] * modes[b][None]]
where the time goes in v1:
time: 65.7 us; the launch traced here: 65.6 us
  Pallas kernels  62.4 us (95%)
  local copies, waits for them, and re-layouts  3.16 us (5%)
    pallas_call x1, Pallas kernels, local(): pl.pallas_call(functools.partial(kernel, (rows, cols, fields, nx, ny, nz)...  62.4 us
    unnamed x1, local copies, waits for them, and re-layouts  3.16 us

profile of v1, /device:TPU:0, one launch (start us, length us, event | category | flops | bytes accessed | tf_op | source)
XLA Modules:
  0.0 65.6 jit_solution(13682978523638818393)
XLA Ops:
  0.0 62.4 %shard_map.82 = f32[2,32,64,128]{3,2,1,0:T(8,128)} custom-call(f32[2,2]{1,0:T(2,128)} %coupling_ref.1, f32[256]{0:T(256)} %sx_ref.1, f32[2,1024,256]{2,1,0:T(8,128)} %bitcast.5, bf16[256,768]{1,0:T(8,128)(2,1)} %constant.6.clone.hx_hbm, bf16[256,768]{1,0:T(8,128)(2,1)} %constant.7.clone.hy_hbm, bf16[256,256]{1,0:T(8,128)(2,1)} %constant.8.clone.hz_hbm, ...), custom_call_target="tpu_custom_call" | custom-call | tf_op jit(solution)/shard_map/pallas_call | solution.py:249
  62.4 3.2 %copy.10 = f32[2,32,64,128]{3,2,1,0:T(8,128)} copy(f32[2,32,64,128]{3,2,1,0:T(8,128)} %shard_map.82) | data formatting | bytes 4194304

commit v2 on v1

--- a/solution.py
+++ b/solution.py
@@ -60,9 +60,9 @@
     return parts
 
 
-def kernel(sizes, coupling_ref, sx_ref, a_hbm, hx_hbm, hy_hbm, hz_hbm, sy_ref, sz_ref, o_hbm,
-           a_ref, hx_ref, hy_ref, hz_ref, sy_rows, m_ref, o_ref, t_ref, r_ref, v_ref, w_ref,
-           load_a, load_h, store_o, send_row, recv_row, send_col, recv_col, own_row, own_col):
+def kernel(sizes, coupling_ref, sx_ref, a_hbm, hx_hbm, hy_hbm, hz_hbm, sy_ref, sz_ref, o_ref,
+           a_ref, hx_ref, hy_ref, hz_ref, sy_rows, m_ref, t_ref, r_ref, v_ref, w_ref,
+           load_a, load_h, send_row, recv_row, send_col, recv_col, own_row, own_col):
     rows, cols, fields, nx, ny, nz = sizes
     share_y = ny // cols
     groups = LANES // (nz // cols)
@@ -117,24 +117,30 @@
         return pltpu.make_async_copy(v_ref.at[i, col], w_ref.at[i, col], own_col.at[i])
 
     tables[0].wait()
+    span = rows * SUB
+    arrived = set()
     for f in range(fields):
-        for n in range(pieces):
-            load(f, n).wait()
-            high, low = halves(a_ref[f, n * width:(n + 1) * width, :])
-            part = lax.dot_general(
-                hx_ref[...], jnp.concatenate([high, high, low], axis=1),
-                (((1,), (1,)), ((), ())), preferred_element_type=jnp.float32)
-            part = part.reshape(rows, chunks, SUB, width)
-            for j in range(chunks):
-                for b in range(per_dot):
-                    at = (n * per_dot + b) * SUB
-                    t_ref[f * chunks + j, :, at:at + SUB, :] = part[:, j, :, b * LANES:(b + 1) * LANES]
-        if f == 0:
-            pl.semaphore_wait(barrier, rows + cols - 2)
-        for j in range(chunks):
-            for step in range(rows - 1, 0, -1):
-                row_copy(f * chunks + j, step).start()
-            own_row_copy(f * chunks + j).start()
+        for low_j, top_j in ((0, 1), (1, chunks)) if f == 0 else ((0, chunks),):
+            for n in range(pieces):
+                if (f, n) not in arrived:
+                    load(f, n).wait()
+                    arrived.add((f, n))
+                high, low = halves(a_ref[f, n * width:(n + 1) * width, :])
+                part = lax.dot_general(
+                    hx_ref[low_j * span:top_j * span, :], jnp.concatenate([high, high, low], axis=1),
+                    (((1,), (1,)), ((), ())), preferred_element_type=jnp.float32)
+                part = part.reshape(top_j - low_j, rows, SUB, width)
+                for j in range(low_j, top_j):
+                    for b in range(per_dot):
+                        at = (n * per_dot + b) * SUB
+                        t_ref[f * chunks + j, :, at:at + SUB, :] = part[
+                            j - low_j, :, :, b * LANES:(b + 1) * LANES]
+            if not f and not low_j:
+                pl.semaphore_wait(barrier, rows + cols - 2)
+            for j in range(low_j, top_j):
+                for step in range(rows - 1, 0, -1):
+                    row_copy(f * chunks + j, step).start()
+                own_row_copy(f * chunks + j).start()
 
     tables[1].wait()
 
@@ -188,10 +194,6 @@
 
     lax.fori_loop(0, total - chunks, z_step, 0)
 
-    def store(j):
-        at = pl.ds(j * SUB, SUB)
-        return pltpu.make_async_copy(o_ref.at[:, at], o_hbm.at[:, at], store_o.at[j])
-
     def last_step(j, carry):
         last = modes_of(total - chunks + j)
         lines_y = sy_rows[pl.ds(col * share_y, share_y), :]
@@ -205,7 +207,6 @@
                 for b in range(1, fields):
                     mixed = mixed + coupling_ref[f, b] * old[b]
                 o_ref[f, j * SUB + k] = weight * old[f] + (1.0 - weight) * mixed
-        store(j).start()
         return carry
 
     lax.fori_loop(0, chunks, last_step, 0)
@@ -218,8 +219,6 @@
         return carry
 
     lax.fori_loop(0, total, drain, 0)
-    for j in range(chunks):
-        store(j).wait()
 
 
 def local(rows, cols, species, coupling, symbol_x, symbol_y, symbol_z):
@@ -230,7 +229,8 @@
     blocks = near_y // groups
     total = fields * share_x // SUB
 
-    high, low = halves_of(mode_table(nx))
+    order = np.arange(nx).reshape(rows, share_x // SUB, SUB).transpose(1, 0, 2).reshape(-1)
+    high, low = halves_of(mode_table(nx)[order])
     hx = np.concatenate([high, low, high], axis=1)
     order = np.arange(ny).reshape(rows, blocks, groups).transpose(2, 0, 1).reshape(-1)
     high, low = halves_of(mode_table(ny)[:, order])
@@ -248,9 +248,9 @@
     chunks = total // fields
     return pl.pallas_call(
         functools.partial(kernel, (rows, cols, fields, nx, ny, nz)),
-        out_shape=jax.ShapeDtypeStruct((fields, share_x, share_y, nz), f32),
+        out_shape=pltpu.VMEM((fields, share_x, share_y, nz), f32),
         in_specs=[smem, smem, hbm, hbm, hbm, hbm, vmem, vmem],
-        out_specs=hbm,
+        out_specs=vmem,
         scratch_shapes=[
             pltpu.VMEM(lines.shape, f32),
             pltpu.VMEM(hx.shape, hx.dtype),
@@ -258,18 +258,17 @@
             pltpu.VMEM(hz.shape, hz.dtype),
             pltpu.VMEM((ny, LANES), f32),
             pltpu.VMEM((max(total - chunks, 1), SUB * share_y, nz), f32),
-            pltpu.VMEM((fields, share_x, share_y, nz), f32),
             pltpu.VMEM((total, rows, blocks * SUB, LANES), f32),
             pltpu.VMEM((total, rows * blocks * SUB, LANES), f32),
             pltpu.VMEM((total, cols, SUB // groups * share_y, LANES), f32),
             pltpu.VMEM((total, cols, SUB // groups * share_y, LANES), f32),
-            dma((fields, blocks // 2)), dma((3,)), dma((chunks,)),
+            dma((fields, blocks // 2)), dma((3,)),
             dma((total, rows)), dma((total, rows)),
             dma((total, cols)), dma((total, cols)),
             dma((total,)), dma((total,)),
         ],
         compiler_params=pltpu.CompilerParams(
-            collective_id=0, has_side_effects=True, vmem_limit_bytes=60 * 2**20),
+            collective_id=0, has_side_effects=True, vmem_limit_bytes=56 * 2**20),
     )(coupling, symbol_x, lines, jnp.asarray(hx), jnp.asarray(hy), jnp.asarray(hz),
       symbol_y[None, :], symbol_z[None, :])
 

time: 65.7 us -> 63 us (0.959)
  local copies, waits for them, and re-layouts: 3.16 us -> 1.32 us
  Pallas kernels: 62.4 us -> 61.5 us
    unnamed x1, local copies, waits for them, and re-layouts: 3.16 us -> 1.32 us
    pallas_call x1, Pallas kernels: 62.4 us -> 61.5 us  [local(): pl.pallas_call(functools.partial(kernel, (rows, cols, fields, nx, ny, nz)...]
where the time goes in v2:
time: 63 us; the launch traced here: 62.8 us
  Pallas kernels  61.5 us (98%)
  local copies, waits for them, and re-layouts  1.32 us (2%)
    pallas_call x1, Pallas kernels, local(): pl.pallas_call(functools.partial(kernel, (rows, cols, fields, nx, ny, nz)...  61.5 us
    unnamed x1, local copies, waits for them, and re-layouts  1.32 us

profile of v2, /device:TPU:0, one launch (start us, length us, event | category | flops | bytes accessed | tf_op | source)
XLA Modules:
  0.0 62.8 jit_solution(12696575255046528285)
XLA Ops:
  0.0 61.5 %shard_map.82 = f32[2,32,64,128]{3,2,1,0:T(8,128)S(1)} custom-call(f32[2,2]{1,0:T(2,128)} %coupling_ref.1, f32[256]{0:T(256)} %sx_ref.1, f32[2,1024,256]{2,1,0:T(8,128)} %bitcast.5, bf16[256,768]{1,0:T(8,128)(2,1)} %constant.6.clone.hx_hbm, bf16[256,768]{1,0:T(8,128)(2,1)} %constant.7.clone.hy_hbm, bf16[256,256]{1,0:T(8,128)(2,1)} %constant.8.clone.hz_hbm, ...), custom_call_target="tpu_custom_call" | custom-call | tf_op jit(solution)/shard_map/pallas_call | solution.py:249
  61.5 1.3 %copy.10 = f32[2,32,64,128]{3,2,1,0:T(8,128)} copy(f32[2,32,64,128]{3,2,1,0:T(8,128)S(1)} %shard_map.82) | data formatting | bytes 4194304
